TPU v7x, 32 devices: a whole 2x2x4 slice. The times are simulated.
32 devices in a mesh: seq: 8 (over z, y), chan: 4 (over x, core).
Axes of the slice: x: 2, y: 2, z: 4, core: 2. Of those that a mesh axis runs over, the one named last changes fastest.
Arguments:
- hidden_in: bfloat16 [1024, 2048], P('seq', 'chan'), may hold values from -6 to 6
- norm_gain: float32 [2048], replicated, may hold values from 0.5 to 1.5
- in_weight: bfloat16 [2048, 2, 4096], P('seq', None, 'chan'), may hold values from -0.125 to 0.125
- conv_weight: float32 [2, 4, 4096], P(None, None, 'chan'), may hold values from -3 to 3
- conv_bias: float32 [2, 4096], P(None, 'chan'), may hold values from -0.5 to 0.5
- proj_weight: bfloat16 [2, 4096, 160], P(None, 'chan'), may hold values from -0.1875 to 0.1875
- step_weight: bfloat16 [2, 128, 4096], P(None, None, 'chan'), may hold values from -0.5 to 0.5
- decay_rate: float32 [2, 4096], P(None, 'chan'), may hold values from 0.00024414062 to 0.25
- skip_gain: float32 [2, 4096], P(None, 'chan'), may hold values from 0.5 to 1.5
- out_weight: bfloat16 [4096, 2048], P('chan', 'seq'), may hold values from -0.09375 to 0.09375
Outputs:
- mixed: bfloat16 [1024, 2048], P('seq', 'chan')
All inputs are finite; a program needn't handle non-finite values.
Results may differ from a plain program's by a relative error of at most 0.0095.
Values may be sent and summed in bfloat16 or wider, within the bound.
No kernel may reach another device: no remote copies, remote signals or barrier semaphores. Data moves between devices by JAX's collectives and lax.ppermute only.
A program may use at most 128 MiB of HBM per device.

v0:
```python
import jax
import jax.numpy as jnp
from jax import lax
from jax.sharding import PartitionSpec as P

STATE = 16
WIDTH = 4


def with_halo(block, sides, width):
    for axis, dim in sides:
        count = lax.axis_size(axis)
        forward = [(i, i + 1) for i in range(count - 1)]
        backward = [(target, source) for source, target in forward]
        low = lax.ppermute(
            lax.slice_in_dim(block, block.shape[dim] - width, None, axis=dim), axis, forward
        )
        high = lax.ppermute(lax.slice_in_dim(block, 0, width, axis=dim), axis, backward)
        block = jnp.concatenate([low, block, high], axis=dim)
    return block


def entering(array, axis, combine, identity, reverse):
    devices, here = (lax.axis_size(axis), lax.axis_index(axis))
    everything = jax.tree.map(lambda part: lax.all_gather(part, axis), array)
    start = jax.tree.map(
        lambda part, zero: jnp.broadcast_to(jnp.asarray(zero, part.dtype), part.shape),
        array,
        identity,
    )

    def hop(k, before):
        at = devices - 1 - k if reverse else k
        reached = at > here if reverse else at < here
        new = combine(before, jax.tree.map(lambda part: part[at], everything))
        return jax.tree.map(lambda a, b: jnp.where(reached, a, b), new, before)

    return lax.fori_loop(0, devices, hop, start)


def conv_taps(padded, conv_weight, conv_bias, length):
    reach = conv_weight.shape[1] - 1
    forward = jnp.zeros((length, padded.shape[1]), jnp.float32) + conv_bias[0][None, :]
    backward = jnp.zeros((length, padded.shape[1]), jnp.float32) + conv_bias[1][None, :]
    for offset in range(reach + 1):
        forward = forward + conv_weight[0, offset][None, :] * padded[offset : offset + length]
        begin = 2 * reach - offset
        backward = backward + conv_weight[1, offset][None, :] * padded[begin : begin + length]
    return jax.nn.silu(jnp.stack([forward, backward])).astype(jnp.bfloat16)


def sweep(drive_values, key_rows, query_rows, epsilon, initial, reverse, keeping):
    product = jnp.ones(initial.shape, jnp.float32)

    def advance(carry, current):
        product, state = carry
        drive_row, key_row, query_row, eps_row = current
        decay = 1.0 - eps_row[None, :] * (key_row * key_row)[:, None]
        state = decay * state + key_row[:, None] * (eps_row * drive_row)[None, :]
        product = decay * product
        if keeping == "reads":
            output = jnp.sum(query_row[:, None] * state, axis=0)
        else:
            output = None
        return ((product, state), output)

    (product, state), outputs = lax.scan(
        advance,
        (product, initial),
        (drive_values, key_rows, query_rows, epsilon),
        reverse=reverse,
        unroll=16,
    )
    return (product, state, outputs)


def combine(earlier, latter):
    return (latter[0] * earlier[0], latter[0] * earlier[1] + latter[1])


def per_device(
    hidden_in,
    norm_gain,
    in_weight,
    conv_weight,
    conv_bias,
    proj_weight,
    step_weight,
    decay_rate,
    skip_gain,
    out_weight,
):
    gathered = lax.all_gather(hidden_in, "chan", axis=1, tiled=True).astype(jnp.float32)
    normed = (
        gathered
        * lax.rsqrt(jnp.mean(gathered * gathered, axis=1, keepdims=True) + 1e-05)
        * norm_gain[None, :]
    ).astype(jnp.bfloat16)
    row_count = normed.shape[0]
    channels = in_weight.shape[2]
    piece = lax.all_gather(in_weight, "seq", axis=0, tiled=True)
    projected = jnp.dot(
        normed, piece.reshape(piece.shape[0], 2 * channels), preferred_element_type=jnp.float32
    )
    projected = projected.astype(jnp.bfloat16).reshape(row_count, 2, channels)
    branch = projected[:, 0, :]
    gate_half = projected[:, 1, :].astype(jnp.float32)
    padded = with_halo(branch, (("seq", 0),), WIDTH - 1).astype(jnp.float32)
    driven = conv_taps(padded, conv_weight, conv_bias, row_count)
    partial_value = jnp.einsum(
        "dte,def->tdf", driven, proj_weight, preferred_element_type=jnp.float32
    )
    features = lax.psum(partial_value, "chan")
    key_rows = features[:, :, :STATE]
    query_rows = features[:, :, STATE : 2 * STATE]
    low_rank = features[:, :, 2 * STATE :].astype(jnp.bfloat16)
    step_size = jnp.einsum(
        "tdr,dre->tde", low_rank, step_weight, preferred_element_type=jnp.float32
    )
    beta_rows = 2.0 * decay_rate[None, :, :] * jax.nn.sigmoid(step_size)
    epsilon = beta_rows / (1.0 + beta_rows * jnp.sum(key_rows * key_rows, axis=2, keepdims=True))
    drive_values = driven.astype(jnp.float32)
    zero_state = jnp.zeros((STATE, channels), jnp.float32)
    keeping = "summary"
    passes = [
        sweep(
            drive_values[direction],
            key_rows[:, direction],
            query_rows[:, direction],
            epsilon[:, direction],
            zero_state,
            direction == 1,
            keeping,
        )
        for direction in range(2)
    ]
    identity = (jnp.ones((STATE, channels), jnp.float32), zero_state)
    incoming_forward = entering((passes[0][0], passes[0][1]), "seq", combine, identity, False)[1]
    incoming_reverse = entering((passes[1][0], passes[1][1]), "seq", combine, identity, True)[1]
    incoming = [incoming_forward, incoming_reverse]
    total = jnp.zeros((row_count, channels), jnp.float32)
    for direction in range(2):
        reads = sweep(
            drive_values[direction],
            key_rows[:, direction],
            query_rows[:, direction],
            epsilon[:, direction],
            incoming[direction],
            direction == 1,
            "reads",
        )[2]
        total = total + reads + skip_gain[direction][None, :] * drive_values[direction]
    combined = (total * jax.nn.silu(gate_half)).astype(jnp.bfloat16)
    partial_out = jnp.dot(
        combined,
        lax.all_gather(out_weight, "seq", axis=1, tiled=True),
        preferred_element_type=jnp.float32,
    )
    summed = lax.psum(partial_out, "chan")
    share_width = summed.shape[1] // lax.axis_size("chan")
    share = lax.dynamic_slice_in_dim(summed, lax.axis_index("chan") * share_width, share_width, 1)
    return share.astype(jnp.bfloat16)


def solution(mesh):
    in_specs = (
        P("seq", "chan"),
        P(),
        P("seq", None, "chan"),
        P(None, None, "chan"),
        P(None, "chan"),
        P(None, "chan", None),
        P(None, None, "chan"),
        P(None, "chan"),
        P(None, "chan"),
        P("chan", "seq"),
    )
    out_specs = P("seq", "chan")
    return jax.shard_map(
        per_device, mesh=mesh, in_specs=in_specs, out_specs=out_specs, check_vma=False
    )
```

profile of v0, /device:TPU:0, one launch (start us, length us, event | category | flops | bytes accessed | tf_op | source)
XLA Modules:
  0.0 489.7 jit_solution(10717089666315897083)
XLA Ops:
  7.3 8.9 %all_gather.33 = bf16[128,2048]{1,0:T(8,128)(2,1)S(1)} all-gather(bf16[128,512]{1,0:T(8,128)(2,1)} %param.22), channel_id=1, replica_groups=mesh['seq'=8,'chan'=4] {'chan'}, dimensions={1}, use_global_device_ids=true | all-gather | bytes 655360 | tf_op jit(solution)/shard_map/all_gather | solution.py:93
  18.1 118.6 %all-gather.7.cloned.1.call-done = bf16[2048,2,1024]{2,1,0:T(2,128)(2,1)} async-done(((bf16[256,2,1024]{2,1,0:T(2,128)(2,1)}), bf16[2048,2,1024]{2,1,0:T(2,128)(2,1)}) %all-gather.7.cloned.1.call-update) | async-done | bytes 8388624 | tf_op jit(solution)/shard_map/all_gather | solution.py:101
  136.7 10.1 %copy.42 = bf16[256,8,2,1024]{3,1,2,0:T(8,128)(2,1)} copy(bf16[256,8,2,1024]{3,2,1,0:T(2,128)(2,1)} %bitcast.855) | data formatting | bytes 16777216
  146.8 4.7 convolution_convert_fusion
  153.3 4.5 collective-permute-start
  163.2 30.7 %all-reduce.3.cloned.1.call-done = f32[128,2,160]{0,2,1:T(8,128)} async-done(((f32[128,2,160]{0,2,1:T(8,128)}), f32[128,2,160]{0,2,1:T(8,128)}) %all-reduce.3.cloned.1.call-update) | async-done | bytes 163856 | tf_op jit(solution)/shard_map/psum | solution.py:113
  199.1 22.7 %while.92 = (s32[]{:T(128)}, f32[16,1024]{1,0:T(8,128)S(1)}, f32[16,1024]{1,0:T(8,128)S(1)}, f32[8,16,1024]{2,1,0:T(8,128)}, f32[8,16,16]{2,1,0:T(8,128)S(1)}, /...) while((s32[]{:T(128)}, f32[16,1024]{1,0:T(8,128)S(1)}, ...), condition=%wide.region_26.27_spmd.clone, body=%wide.region_25.26_spmd.clone.sunk | while | flops 2146579 | bytes 924200 | solution.py:67
  199.1 2.0 constant_dynamic-slice_fusion.231
  202.1 2.0 constant_dynamic-slice_fusion.231
  207.8 1.8 constant_dynamic-slice_fusion.231
  210.6 2.0 constant_dynamic-slice_fusion.231
  213.5 2.0 constant_dynamic-slice_fusion.231
  219.2 1.8 constant_dynamic-slice_fusion.231
  221.8 9.5 %while.90 = (s32[]{:T(128)}, f32[16,1024]{1,0:T(8,128)S(1)}, f32[16,1024]{1,0:T(8,128)S(1)}, f32[8,16,1024]{2,1,0:T(8,128)S(1)}, f32[8,16,16]{2,1,0:T(8,128)S(1)...) while((s32[]{:T(128)}, f32[16,1024]{1,0:T(8,128)S(1)}, ...), condition=%wide.region_4.5_spmd.clone, body=%wide.region_3.4_spmd.clone.sunk | while | flops 2146578 | bytes 924180 | solution.py:67
  231.3 37.0 %all-gather.1 = f32[128,1024]{1,0:T(8,128)} all-gather(f32[16,1024]{1,0:T(8,128)S(1)} %get-tuple-element.566), channel_id=3, replica_groups=mesh['seq'=8,'chan'=4] {'seq'}, dimensions={0}, use_global_device_ids=true | all-gather | bytes 589824 | tf_op jit(solution)/shard_map/all_gather | solution.py:25
  268.3 34.7 %all-gather.3 = f32[128,1024]{1,0:T(8,128)} all-gather(f32[16,1024]{1,0:T(8,128)S(1)} %get-tuple-element.570), channel_id=5, replica_groups=mesh['seq'=8,'chan'=4] {'seq'}, dimensions={0}, use_global_device_ids=true | all-gather | bytes 589824 | tf_op jit(solution)/shard_map/all_gather | solution.py:25
  303.0 33.4 %all-gather = f32[128,1024]{1,0:T(8,128)} all-gather(f32[16,1024]{1,0:T(8,128)S(1)} %get-tuple-element.565), channel_id=2, replica_groups=mesh['seq'=8,'chan'=4] {'seq'}, dimensions={0}, use_global_device_ids=true | all-gather | bytes 589824 | tf_op jit(solution)/shard_map/all_gather | solution.py:25
  336.4 7.5 %while.91 = (s32[]{:T(128)}, f32[16,1024]{1,0:T(8,128)S(1)}, s32[]{:T(128)}, f32[8,16,1024]{2,1,0:T(8,128)}, f32[8,16,1024]{2,1,0:T(8,128)}, /*index=5*/s32[]{:T(128)}, s32[]{:T(128)}) while((s32[]{:T(128)}, f32[16,1024]{1,0:T(8,128)S(1)}, s32[]{:T(128)}, f32[8,16,1024]{2,1,0:T(8,128)}, f32[8,16,1024]{2,1,0:T(8,128)}, ...), condition=%wide.region_6.7_spmd.clone, body=%wide.region_5.6_spmd.clone.sunk | while | flops 65540 | bytes 262253 | solution.py:38
  343.9 33.6 %all-gather.2 = f32[128,1024]{1,0:T(8,128)} all-gather(f32[16,1024]{1,0:T(8,128)S(1)} %get-tuple-element.569), channel_id=4, replica_groups=mesh['seq'=8,'chan'=4] {'seq'}, dimensions={0}, use_global_device_ids=true | all-gather | bytes 589824 | tf_op jit(solution)/shard_map/all_gather | solution.py:25
  377.5 7.5 %while.93 = (s32[]{:T(128)}, f32[16,1024]{1,0:T(8,128)S(1)}, s32[]{:T(128)}, f32[8,16,1024]{2,1,0:T(8,128)}, f32[8,16,1024]{2,1,0:T(8,128)}, /*index=5*/s32[]{:T(128)}, s32[]{:T(128)}, s32[]{:T(128)}, s32[]{:T(128)}) while((s32[]{:T(128)}, f32[16,1024]{1,0:T(8,128)S(1)}, s32[]{:T(128)}, f32[8,16,1024]{2,1,0:T(8,128)}, ...), condition=%wide.region_28.29_spmd.clone, body=%wide.region_27.28_spmd.clone.sunk | while | flops 65544 | bytes 262315 | solution.py:38
  385.9 33.0 %while.89 = (s32[]{:T(128)}, f32[16,1024]{1,0:T(8,128)S(1)}, f32[8,16,1024]{2,1,0:T(8,128)}, f32[8,16,1024]{2,1,0:T(8,128)}, f32[8,16,16]{2,1,0:T(8,128)S(1)}, /...) while((s32[]{:T(128)}, f32[16,1024]{1,0:T(8,128)S(1)}, ...), condition=%wide.region_46.47_spmd, body=%wide.region_29.46_spmd.sunk | while | flops 2408722 | bytes 2033121 | solution.py:67
  386.1 2.0 constant_dynamic-slice_fusion.229
  390.3 2.0 constant_dynamic-slice_fusion.229
  394.6 1.8 constant_dynamic-slice_fusion.229
  398.6 1.8 constant_dynamic-slice_fusion.229
  402.6 2.0 constant_dynamic-slice_fusion.229
  406.8 2.0 constant_dynamic-slice_fusion.229
  411.0 1.8 constant_dynamic-slice_fusion.229
  415.0 1.8 constant_dynamic-slice_fusion.229
  418.9 32.4 %while.88 = (s32[]{:T(128)}, f32[16,1024]{1,0:T(8,128)S(1)}, f32[8,16,1024]{2,1,0:T(8,128)S(1)}, f32[8,16,1024]{2,1,0:T(8,128)S(1)}, f32[8,16,16]{2,1,0:T(8,128)...) while((s32[]{:T(128)}, f32[16,1024]{1,0:T(8,128)S(1)}, ...), condition=%wide.region_24.25_spmd, body=%wide.region_7.24_spmd.sunk | while | flops 2490641 | bytes 2106965 | solution.py:67
  452.8 2.9 fusion.342
  455.7 26.7 %all-reduce.4 = bf16[128,2048]{1,0:T(8,128)(2,1)S(1)} all-reduce(f32[128,2048]{1,0:T(8,128)S(1)} %fusion.342), channel_id=1, replica_groups=mesh['seq'=8,'chan'=4] {'chan'}, use_global_device_ids=true, to_apply=%region_47.48 | all-reduce | flops 262144 | bytes 1572864 | tf_op jit(solution)/shard_map/psum | solution.py:159
  (853 shorter events, 97.4 us)
Async XLA Ops:
  6.5 153.8 %copy-start = (bf16[2,1024,160]{1,2,0:T(8,128)(2,1)S(1)}, bf16[2,1024,160]{1,2,0:T(8,128)(2,1)}, u32[]{:S(2)}) copy-start(bf16[2,1024,160]{1,2,0:T(8,128)(2,1)} %param.27) | copy-start | bytes 1966084
  6.5 130.2 %all-gather.7.cloned.1.call-start = ((), (), s32[]{:S(2)}) async-start(), calls=%async_computation | async-start | bytes 9437184 | tf_op jit(solution)/shard_map/all_gather | solution.py:101
  7.3 186.6 %all-reduce.3.cloned.1.call-start = ((), (), s32[]{:S(2)}) async-start(), calls=%async_computation.1 | async-start | bytes 327680 | tf_op jit(solution)/shard_map/psum | solution.py:113
  136.7 10.1 %copy-start.4 = (f32[2048]{0:T(1024)S(1)}, f32[2048]{0:T(1024)}, u32[]{:S(2)}) copy-start(f32[2048]{0:T(1024)} %param.23) | copy-start | bytes 24580
  151.5 10.6 %copy-start.5 = (f32[2,1024]{1,0:T(2,128)S(1)}, f32[2,1024]{1,0:T(2,128)}, u32[]{:S(2)}) copy-start(f32[2,1024]{1,0:T(2,128)} %param.29) | copy-start | bytes 24580
  151.5 10.7 %copy-start.6 = (f32[2,1024]{1,0:T(2,128)S(1)}, f32[2,1024]{1,0:T(2,128)}, u32[]{:S(2)}) copy-start(f32[2,1024]{1,0:T(2,128)} %param.30) | copy-start | bytes 24580
  152.0 7.5 %collective-permute-start.1 = (bf16[3,1024]{1,0:T(4,128)(2,1)S(1)}, bf16[3,1024]{1,0:T(4,128)(2,1)S(1)}, u32[]{:S(2)}, u32[]{:S(2)}) collective-permute-start(bf16[3,1024]{1,0:T(4,128)(2,1)S(1)} %bitcast.1151), channel_id=1, source_target_pairs={{4,0},{8,4},{12,8},{16,12},{20,16},{24,20},{28,24},{5,1},{9,5},{13... | collective-permute-start | bytes 18440 | tf_op jit(solution)/shard_map/ppermute | solution.py:18
  153.3 6.2 %collective-permute-start = (bf16[3,1024]{1,0:T(4,128)(2,1)S(1)}, bf16[3,1024]{1,0:T(4,128)(2,1)S(1)}, u32[]{:S(2)}, u32[]{:S(2)}) collective-permute-start(bf16[3,1024]{1,0:T(4,128)(2,1)S(1)} %bitcast.1150), channel_id=1, source_target_pairs={{0,4},{4,8},{8,12},{12,16},{16,20},{20,24},{24,28},{1,5},{5,9},{9,... | collective-permute-start | bytes 18440 | tf_op jit(solution)/shard_map/ppermute | solution.py:15
  161.4 291.4 %all-gather.9.cloned.1.call-start = ((), (), s32[]{:S(2)}) async-start(), calls=%async_computation.2 | async-start | bytes 4718592 | tf_op jit(solution)/shard_map/all_gather | solution.py:156
  163.2 35.9 %copy-start.1 = (f32[16,1024]{1,0:T(8,128)S(1)}, f32[16,1024]{1,0:T(8,128)}, u32[]{:S(2)}) copy-start(f32[16,1024]{1,0:T(8,128)} %custom-call.4) | copy-start | bytes 196612
  163.2 35.9 %copy-start.2 = (f32[16,1024]{1,0:T(8,128)S(1)}, f32[16,1024]{1,0:T(8,128)}, u32[]{:S(2)}) copy-start(f32[16,1024]{1,0:T(8,128)} %custom-call.3) | copy-start | bytes 196612
  231.3 154.6 %copy-start.3 = (f32[8,16,16]{2,1,0:T(8,128)}, f32[8,16,16]{2,1,0:T(8,128)S(1)}, u32[]{:S(2)}) copy-start(f32[8,16,16]{2,1,0:T(8,128)S(1)} %get-tuple-element.2563) | copy-start | bytes 24580
Sparse Core Ops, SparseCore 0:
  9.5 127.1 all-gather.6
  161.5 32.3 all-reduce.2
  195.9 86.4 all-gather.8
where the time goes:
time: 494 us; the launch traced here: 490 us
  blocking collectives  174 us (35%)
  waiting for transfers between devices  151 us (31%)
  local copies, waits for them, and re-layouts  69.2 us (14%)
  other arithmetic  59.8 us (12%)
  between operations  13.4 us (3%)
  matrix products  10.3 us (2%)
  loops' own time  6.06 us (1%)
  starting transfers between devices  5.92 us (1%)
    all_gather x4, blocking collectives, entering(): everything = jax.tree.map(lambda part: lax.all_gather(part, axis), array)  139 us
    all_gather x1, waiting for transfers between devices, per_device(): piece = lax.all_gather(in_weight, 'seq', axis=0, tiled=True)  119 us
    slice x32, local copies, waits for them, and re-layouts, sweep(): lax.scan(advance, (product, initial), (drive_values, key_rows, query_rows...  34.3 us
    psum x1, waiting for transfers between devices, per_device(): features = lax.psum(partial_value, 'chan')  30.7 us
    psum x1, blocking collectives, per_device(): summed = lax.psum(partial_out, 'chan')  26.7 us
    reduce_sum x136, other arithmetic, advance(): output = jnp.sum(query_row[:, None] * state, axis=0)  17.7 us
    select_n x16, other arithmetic, hop(): return jax.tree.map(lambda a, b: jnp.where(reached, a, b), new, before)  14.6 us
    mul x32, other arithmetic, advance(): decay = 1.0 - eps_row[None, :] * (key_row * key_row)[:, None]  12.7 us
  transfers between devices with their start and end apart: 5, of which 2 were waited for; matrix products, arithmetic and copies ran while one was open for 24% of the time, Pallas kernels for 0%

commit v1 on v0

--- a/solution.py
+++ b/solution.py
@@ -5,6 +5,15 @@
 
 STATE = 16
 WIDTH = 4
+
+
+def added_up(x, mesh_axis):
+    size = lax.axis_size(mesh_axis)
+    total, hop = (x, 1)
+    while hop < size:
+        total = total + lax.ppermute(total, mesh_axis, [(i, i ^ hop) for i in range(size)])
+        hop = 2 * hop
+    return total
 
 
 def with_halo(block, sides, width):
@@ -110,7 +119,7 @@
     partial_value = jnp.einsum(
         "dte,def->tdf", driven, proj_weight, preferred_element_type=jnp.float32
     )
-    features = lax.psum(partial_value, "chan")
+    features = added_up(partial_value, "chan")
     key_rows = features[:, :, :STATE]
     query_rows = features[:, :, STATE : 2 * STATE]
     low_rank = features[:, :, 2 * STATE :].astype(jnp.bfloat16)

time: 494 us -> 510 us (1.032)
  other arithmetic: 59.8 us -> 103 us
  waiting for transfers between devices: 151 us -> 125 us
    psum x1 -> x0, waiting for transfers between devices: 30.7 us -> none  [per_device(): features = lax.psum(partial_value, 'chan')]
    mul x32, other arithmetic: 12.7 us -> 34.5 us  [advance(): decay = 1.0 - eps_row[None, :] * (key_row * key_row)[:, None]]
    add x16, other arithmetic: 5.87 us -> 16.9 us  [advance(): state = decay * state + key_row[:, None] * (eps_row * drive_row)[None, :]]
    mul x16, other arithmetic: 3.1 us -> 13.9 us  [advance(): product = decay * product]
    mul x16, local copies, waits for them, and re-layouts: 8.66 us -> 16.3 us  [advance(): output = jnp.sum(query_row[:, None] * state, axis=0)]
    slice x32, local copies, waits for them, and re-layouts: 34.3 us -> 27.3 us  [sweep(): lax.scan(advance, (product, initial), (drive_values, key_rows, query_rows...]
    ppermute x0 -> x2, waiting for transfers between devices: none -> 5.97 us  [added_up(): lax.ppermute(total, mesh_axis, [(i, i ^ hop) for i in range(size)])]
    unnamed x20 -> x12, local copies, waits for them, and re-layouts: 10.5 us -> 11.7 us
  transfers between devices with their start and end apart: 5 -> 6, of which waited for: 2 -> 3; matrix products, arithmetic and copies ran while one was open for 24% -> 36% of each run, Pallas kernels for 0% -> 0%
where the time goes in v1:
time: 510 us; the launch traced here: 504 us
  blocking collectives  169 us (33%)
  waiting for transfers between devices  125 us (25%)
  other arithmetic  103 us (20%)
  local copies, waits for them, and re-layouts  70.1 us (14%)
  between operations  13.7 us (3%)
  matrix products  9.6 us (2%)
  starting transfers between devices  7.54 us (1%)
  loops' own time  5.76 us (1%)
    all_gather x4, blocking collectives, entering(): everything = jax.tree.map(lambda part: lax.all_gather(part, axis), array)  135 us
    all_gather x1, waiting for transfers between devices, per_device(): piece = lax.all_gather(in_weight, 'seq', axis=0, tiled=True)  117 us
    mul x32, other arithmetic, advance(): decay = 1.0 - eps_row[None, :] * (key_row * key_row)[:, None]  34.5 us
    slice x32, local copies, waits for them, and re-layouts, sweep(): lax.scan(advance, (product, initial), (drive_values, key_rows, query_rows...  27.3 us
    psum x1, blocking collectives, per_device(): summed = lax.psum(partial_out, 'chan')  25.2 us
    reduce_sum x136, other arithmetic, advance(): output = jnp.sum(query_row[:, None] * state, axis=0)  17.7 us
    add x16, other arithmetic, advance(): state = decay * state + key_row[:, None] * (eps_row * drive_row)[None, :]  16.9 us
    mul x16, local copies, waits for them, and re-layouts, advance(): output = jnp.sum(query_row[:, None] * state, axis=0)  16.3 us
  transfers between devices with their start and end apart: 6, of which 3 were waited for; matrix products, arithmetic and copies ran while one was open for 36% of the time, Pallas kernels for 0%

profile of v1, /device:TPU:0, one launch (start us, length us, event | category | flops | bytes accessed | tf_op | source)
XLA Modules:
  0.0 504.0 jit_solution(11889414719738010851)
XLA Ops:
  10.5 8.9 %all_gather.33 = bf16[128,2048]{1,0:T(8,128)(2,1)S(1)} all-gather(bf16[128,512]{1,0:T(8,128)(2,1)} %param.22), channel_id=1, replica_groups=mesh['seq'=8,'chan'=4] {'chan'}, dimensions={1}, use_global_device_ids=true | all-gather | bytes 655360 | tf_op jit(solution)/shard_map/all_gather | solution.py:102
  19.6 117.1 %all-gather.7.cloned.1.call-done = bf16[2048,2,1024]{2,1,0:T(2,128)(2,1)} async-done(((bf16[256,2,1024]{2,1,0:T(2,128)(2,1)}), bf16[2048,2,1024]{2,1,0:T(2,128)(2,1)}) %all-gather.7.cloned.1.call-update) | async-done | bytes 8388624 | tf_op jit(solution)/shard_map/all_gather | solution.py:110
  136.7 10.1 %copy.42 = bf16[256,8,2,1024]{3,1,2,0:T(8,128)(2,1)} copy(bf16[256,8,2,1024]{3,2,1,0:T(2,128)(2,1)} %bitcast.855) | data formatting | bytes 16777216
  146.8 4.7 convolution_convert_fusion
  153.3 4.5 collective-permute-start
  163.9 4.6 collective-permute-done.3
  171.4 1.7 add_divide_fusion
  174.0 47.6 %while.92 = (s32[]{:T(128)}, f32[16,1024]{1,0:T(8,128)}, f32[16,1024]{1,0:T(8,128)}, f32[8,16,1024]{2,1,0:T(8,128)}, f32[8,16,16]{2,1,0:T(8,128)}, /*index=5*/f3...) while((s32[]{:T(128)}, f32[16,1024]{1,0:T(8,128)}, ...), condition=%wide.region_25.26_spmd.clone, body=%wide.region_24.25_spmd.clone.sunk | while | flops 2146579 | bytes 924200 | solution.py:76
  181.1 1.9 multiply_add_fusion.53
  183.0 1.6 fusion.367
  187.3 1.9 multiply_add_fusion.53
  189.2 1.6 fusion.367
  193.5 1.9 multiply_add_fusion.53
  195.3 1.6 fusion.367
  199.6 1.9 multiply_add_fusion.53
  201.5 1.6 fusion.367
  205.8 1.9 multiply_add_fusion.53
  207.6 1.6 fusion.367
  211.9 1.9 multiply_add_fusion.53
  213.8 1.6 fusion.367
  218.1 1.9 multiply_add_fusion.53
  221.6 17.0 %while.90 = (s32[]{:T(128)}, f32[16,1024]{1,0:T(8,128)S(1)}, f32[16,1024]{1,0:T(8,128)S(1)}, f32[8,16,1024]{2,1,0:T(8,128)S(1)}, f32[8,16,16]{2,1,0:T(8,128)}, /...) while((s32[]{:T(128)}, f32[16,1024]{1,0:T(8,128)S(1)}, ...), condition=%wide.region_3.4_spmd.clone, body=%wide.region_2.3_spmd.clone.sunk | while | flops 2146578 | bytes 924180 | solution.py:76
  238.6 34.6 %all-gather.1 = f32[128,1024]{1,0:T(8,128)} all-gather(f32[16,1024]{1,0:T(8,128)S(1)} %get-tuple-element.566), channel_id=3, replica_groups=mesh['seq'=8,'chan'=4] {'seq'}, dimensions={0}, use_global_device_ids=true | all-gather | bytes 589824 | tf_op jit(solution)/shard_map/all_gather | solution.py:34
  273.2 33.7 %all-gather.3 = f32[128,1024]{1,0:T(8,128)} all-gather(f32[16,1024]{1,0:T(8,128)} %get-tuple-element.570), channel_id=5, replica_groups=mesh['seq'=8,'chan'=4] {'seq'}, dimensions={0}, use_global_device_ids=true | all-gather | bytes 589824 | tf_op jit(solution)/shard_map/all_gather | solution.py:34
  306.9 33.6 %all-gather = f32[128,1024]{1,0:T(8,128)} all-gather(f32[16,1024]{1,0:T(8,128)S(1)} %get-tuple-element.565), channel_id=2, replica_groups=mesh['seq'=8,'chan'=4] {'seq'}, dimensions={0}, use_global_device_ids=true | all-gather | bytes 589824 | tf_op jit(solution)/shard_map/all_gather | solution.py:34
  340.5 7.5 %while.91 = (s32[]{:T(128)}, f32[16,1024]{1,0:T(8,128)S(1)}, s32[]{:T(128)}, f32[8,16,1024]{2,1,0:T(8,128)}, f32[8,16,1024]{2,1,0:T(8,128)}, /*index=5*/s32[]{:T(128)}, s32[]{:T(128)}) while((s32[]{:T(128)}, f32[16,1024]{1,0:T(8,128)S(1)}, s32[]{:T(128)}, f32[8,16,1024]{2,1,0:T(8,128)}, f32[8,16,1024]{2,1,0:T(8,128)}, ...), condition=%wide.region_5.6_spmd.clone, body=%wide.region_4.5_spmd.clone.sunk | while | flops 65540 | bytes 262253 | solution.py:47
  348.0 33.4 %all-gather.2 = f32[128,1024]{1,0:T(8,128)} all-gather(f32[16,1024]{1,0:T(8,128)} %get-tuple-element.569), channel_id=4, replica_groups=mesh['seq'=8,'chan'=4] {'seq'}, dimensions={0}, use_global_device_ids=true | all-gather | bytes 589824 | tf_op jit(solution)/shard_map/all_gather | solution.py:34
  381.4 7.5 %while.93 = (s32[]{:T(128)}, f32[16,1024]{1,0:T(8,128)S(1)}, s32[]{:T(128)}, f32[8,16,1024]{2,1,0:T(8,128)}, f32[8,16,1024]{2,1,0:T(8,128)}, /*index=5*/s32[]{:T(128)}, s32[]{:T(128)}, s32[]{:T(128)}, s32[]{:T(128)}) while((s32[]{:T(128)}, f32[16,1024]{1,0:T(8,128)S(1)}, s32[]{:T(128)}, f32[8,16,1024]{2,1,0:T(8,128)}, ...), condition=%wide.region_27.28_spmd.clone, body=%wide.region_26.27_spmd.clone.sunk | while | flops 65544 | bytes 262315 | solution.py:47
  389.8 44.7 %while.89 = (s32[]{:T(128)}, f32[16,1024]{1,0:T(8,128)S(1)}, f32[8,16,1024]{2,1,0:T(8,128)}, f32[8,16,1024]{2,1,0:T(8,128)}, f32[8,16,16]{2,1,0:T(8,128)}, /*ind...) while((s32[]{:T(128)}, f32[16,1024]{1,0:T(8,128)S(1)}, ...), condition=%wide.region_45.46_spmd, body=%wide.region_28.45_spmd.sunk | while | flops 2408722 | bytes 2033121 | solution.py:76
  434.5 32.3 %while.88 = (s32[]{:T(128)}, f32[16,1024]{1,0:T(8,128)S(1)}, f32[8,16,1024]{2,1,0:T(8,128)S(1)}, f32[8,16,1024]{2,1,0:T(8,128)S(1)}, f32[8,16,16]{2,1,0:T(8,128)...) while((s32[]{:T(128)}, f32[16,1024]{1,0:T(8,128)S(1)}, ...), condition=%wide.region_23.24_spmd, body=%wide.region_6.23_spmd.sunk | while | flops 2490641 | bytes 2106965 | solution.py:76
  468.4 2.9 fusion.342
  471.3 25.2 %all-reduce.1 = bf16[128,2048]{1,0:T(8,128)(2,1)S(1)} all-reduce(f32[128,2048]{1,0:T(8,128)S(1)} %fusion.342), channel_id=1, replica_groups=mesh['seq'=8,'chan'=4] {'chan'}, use_global_device_ids=true, to_apply=%region_46.47 | all-reduce | flops 262144 | bytes 1572864 | tf_op jit(solution)/shard_map/psum | solution.py:168
  (848 shorter events, 146.7 us)
Async XLA Ops:
  6.5 153.8 %copy-start = (bf16[2,1024,160]{1,2,0:T(8,128)(2,1)S(1)}, bf16[2,1024,160]{1,2,0:T(8,128)(2,1)}, u32[]{:S(2)}) copy-start(bf16[2,1024,160]{1,2,0:T(8,128)(2,1)} %param.27) | copy-start | bytes 1966084
  6.5 130.2 %all-gather.7.cloned.1.call-start = ((), (), s32[]{:S(2)}) async-start(), calls=%async_computation | async-start | bytes 9437184 | tf_op jit(solution)/shard_map/all_gather | solution.py:110
  7.3 461.1 %all-gather.9.cloned.1.call-start = ((), (), s32[]{:S(2)}) async-start(), calls=%async_computation.1 | async-start | bytes 4718592 | tf_op jit(solution)/shard_map/all_gather | solution.py:165
  136.7 10.1 %copy-start.1 = (f32[2048]{0:T(1024)S(1)}, f32[2048]{0:T(1024)}, u32[]{:S(2)}) copy-start(f32[2048]{0:T(1024)} %param.23) | copy-start | bytes 24580
  151.5 9.2 %copy-start.2 = (f32[2,1024]{1,0:T(2,128)S(1)}, f32[2,1024]{1,0:T(2,128)}, u32[]{:S(2)}) copy-start(f32[2,1024]{1,0:T(2,128)} %param.30) | copy-start | bytes 24580
  152.0 7.5 %collective-permute-start.1 = (bf16[3,1024]{1,0:T(4,128)(2,1)S(1)}, bf16[3,1024]{1,0:T(4,128)(2,1)S(1)}, u32[]{:S(2)}, u32[]{:S(2)}) collective-permute-start(bf16[3,1024]{1,0:T(4,128)(2,1)S(1)} %bitcast.1153), channel_id=1, source_target_pairs={{4,0},{8,4},{12,8},{16,12},{20,16},{24,20},{28,24},{5,1},{9,5},{13... | collective-permute-start | bytes 18440 | tf_op jit(solution)/shard_map/ppermute | solution.py:27
  153.3 6.2 %collective-permute-start = (bf16[3,1024]{1,0:T(4,128)(2,1)S(1)}, bf16[3,1024]{1,0:T(4,128)(2,1)S(1)}, u32[]{:S(2)}, u32[]{:S(2)}) collective-permute-start(bf16[3,1024]{1,0:T(4,128)(2,1)S(1)} %bitcast.1152), channel_id=1, source_target_pairs={{0,4},{4,8},{8,12},{12,16},{16,20},{20,24},{24,28},{1,5},{5,9},{9,... | collective-permute-start | bytes 18440 | tf_op jit(solution)/shard_map/ppermute | solution.py:24
  160.7 1.5 collective-permute-start.2
  162.2 6.3 %collective-permute-start.3 = (f32[128,2,160]{0,2,1:T(8,128)S(1)}, f32[128,2,160]{0,2,1:T(8,128)S(1)}, u32[]{:S(2)}, u32[]{:S(2)}) collective-permute-start(f32[128,2,160]{0,2,1:T(8,128)S(1)} %add.591), channel_id=1, source_target_pairs={{0,2},{1,3},{2,0},{3,1},{4,6},{5,7},{6,4},{7,5},{8,10},{9,11},{10,... | collective-permute-start | bytes 491528 | tf_op jit(solution)/shard_map/ppermute | solution.py:14
Sparse Core Ops, SparseCore 0:
  9.5 127.1 all-gather.6
  138.7 72.7 all-gather.8
